TPU v7x, 32 devices: a whole 2x2x4 slice. The times are simulated.
32 devices in a mesh: gx: 4 (over z), gy: 4 (over y, x), gz: 2 (over core).
Axes of the slice: x: 2, y: 2, z: 4, core: 2. Of those that a mesh axis runs over, the one named last changes fastest.
Arguments:
- patch_logits: bfloat16 [4, 4, 2, 24, 20736], P('gx', 'gy', 'gz'), may hold values from -12 to 312
- patch_start: int32 [4, 4, 2, 3], replicated, may hold values from 0 to 112, as said below
- patch_owner: int32 [4, 4, 2], replicated, may hold values from 0 to 15, as said below
Outputs:
- probs: float32 [32, 128, 3, 256], P('gx', 'gy', None, 'gz')
Inputs may be any that keep to these rules, and one draw needn't show every extreme that they name: `patch_start`: entry [i, j, k, d] is the first cell along dimension d of the patch at lattice position (i, j, k): i * 8 - 8 along x (32 and 128 in place of 8 along y and z), moved by at most 4 cells, then moved inward so that the patch lies inside the volume. `patch_owner`: for every k the entries [:, :, k] are the numbers 0 to 15, each once.
All inputs are finite; a program needn't handle non-finite values.
Results may differ from a plain program's by a relative error of at most 0.0003.
Values may be sent and summed in bfloat16 or wider, within the bound.
A program may use at most 128 MiB of HBM per device.

v0:
```python
import functools

import jax
import jax.numpy as jnp
from jax import lax
from jax.experimental import pallas as pl
from jax.experimental.pallas import tpu as pltpu
from jax.sharding import PartitionSpec as P

CLASSES = 3
BX = 8
BY = 32
BZ = 128
HALO = 8
PX = 24
PY = 48
PZ = 144
RIM = PZ - BZ
ROWS = CLASSES + 1
GROUP = 8
FOLD = PY // 2
MESH = pl.DeviceIdType.MESH


def profile(offsets, length, keep=True):
    inside = (offsets >= 0) & (offsets < length) & keep
    centre = (length - 1) / 2.0
    spread = length / 4.0
    values = jnp.exp((offsets.astype(jnp.float32) - centre) ** 2 * (-0.5 / (spread * spread)))
    return jnp.where(inside, values, 0.0)


def corner_of(start_ref, code, lanes_y, layer):
    return [start_ref[code // lanes_y, k, layer, code % lanes_y] for k in range(3)]


def pick_x(lanes_x, place_x, start_x, logits_ref, cells_ref):
    rows = lanes_x * BX
    r = lax.broadcasted_iota(jnp.int32, (rows, PX), 0)
    p = lax.broadcasted_iota(jnp.int32, (rows, PX), 1)
    x = r + place_x * BX
    x = jnp.where(x >= rows, x - rows, x)
    pick = jnp.where(x - start_x == p, 1.0, 0.0).astype(jnp.bfloat16)
    width = GROUP * CLASSES * PZ
    for g in range(PY // GROUP):
        lanes = slice(g * width, (g + 1) * width)
        cells = jnp.dot(pick, logits_ref[:, lanes], preferred_element_type=jnp.float32)
        cells_ref[:, lanes] = cells.astype(jnp.bfloat16)


def lines_of(cells_ref, lines, source, phase):
    k = lax.broadcasted_iota(jnp.int32, (2 * BZ, BZ), 0)
    move = jnp.where(k - phase * RIM == source, 1.0, 0.0).astype(jnp.bfloat16)
    starts = [line * PZ - phase * RIM for line in lines]
    cells = jnp.concatenate([cells_ref[:, at : at + 2 * BZ] for at in starts], axis=0)
    return jnp.dot(cells, move, preferred_element_type=jnp.float32)


def pack_rims(lanes_x, shift_z, cells_ref, sums_ref, out_ref):
    rows = lanes_x * BX
    phases = BZ // RIM
    n = lax.broadcasted_iota(jnp.int32, (2 * BZ, BZ), 1)
    source = n + shift_z + jnp.where(n + shift_z < RIM, BZ, -RIM)
    source = jnp.where(n < RIM, source, -4 * BZ)
    sums_ref[...] = jnp.zeros(sums_ref.shape, jnp.float32)
    for phase in range(phases):
        lines = [i for i in range(PY * CLASSES) if i % phases == phase]
        moved = lines_of(cells_ref, lines, source, phase)
        for i, line in enumerate(lines):
            y, c = divmod(line, CLASSES)
            rim = moved[i * rows : (i + 1) * rows]
            at = RIM * c + BZ // 2 * (y // FOLD)
            rim = pltpu.roll(rim, at, 1) if at else rim
            sums_ref[y % FOLD] = sums_ref[y % FOLD] + rim

    def convert(y, carry):
        sums = sums_ref[y].astype(jnp.bfloat16)
        for t in range(lanes_x):
            out_ref[t, y] = sums[t * BX : (t + 1) * BX]
        return carry

    lax.fori_loop(0, FOLD, convert, 0, unroll=2)


def pack_class(lanes_x, shift_z, c, cells_ref, out_ref):
    rows = lanes_x * BX
    phases = BZ // RIM
    source = lax.broadcasted_iota(jnp.int32, (2 * BZ, BZ), 1) + shift_z
    for phase in range(phases):
        ys = [y for y in range(PY) if (y * CLASSES + c) % phases == phase]
        moved = lines_of(cells_ref, [y * CLASSES + c for y in ys], source, phase)
        moved = moved.astype(jnp.bfloat16)
        for i, y in enumerate(ys):
            for t in range(lanes_x):
                at = i * rows + t * BX
                out_ref[t, y] = moved[at : at + BX]


def blend_kernel(
    lanes_x, lanes_y, lanes_z,
    start_ref, owner_ref, logits_ref, out_ref, along_y_ref, plane_ref, weight_ref,
    cells_ref, sums_ref, pack0, pack1, pack2, pack3, land0, land1, land2, land3, parts, parts_land, rims, rims_land,
    cells_out, cells_in, parts_out, parts_in, rims_out, rims_in,
):
    place_x = lax.axis_index("gx")
    place_y = lax.axis_index("gy")
    place_z = lax.axis_index("gz")

    packed = (pack0, pack1, pack2, pack3)
    cells_land = (land0, land1, land2, land3)

    def ahead(place, d, size):
        return lax.rem(place + d, size)

    barrier = pltpu.get_barrier_semaphore()
    peers = [{"gx": ahead(place_x, d, lanes_x)} for d in range(1, lanes_x)]
    peers += [{"gy": ahead(place_y, d, lanes_y)} for d in range(1, lanes_y)]
    peers += [{"gz": ahead(place_z, d, lanes_z)} for d in (1, lanes_z - 1)]
    for peer in peers:
        pl.semaphore_signal(barrier, inc=1, device_id=peer, device_id_type=MESH)

    code = owner_ref[place_x, place_z, place_y]
    start_x, _, start_z = corner_of(start_ref, code, lanes_y, place_z)
    shift_z = place_z * BZ - start_z
    pick_x(lanes_x, place_x, start_x, logits_ref, cells_ref)

    order = (0, CLASSES) + tuple(range(1, CLASSES))
    far_x = sorted(range(1, lanes_x), key=lambda d: -min(d, lanes_x - d))
    far_y = sorted(range(1, lanes_y), key=lambda d: -min(d, lanes_y - d))
    cell_copies = {
        (c, d): pltpu.make_async_remote_copy(
            src_ref=packed[c].at[d],
            dst_ref=cells_land[c].at[d],
            send_sem=cells_out.at[c, d],
            recv_sem=cells_in.at[c, d],
            device_id={"gx": ahead(place_x, d, lanes_x)},
            device_id_type=MESH,
        )
        for c in order
        for d in far_x
    }
    part_copies = {
        (c, d): pltpu.make_async_remote_copy(
            src_ref=parts.at[c, d],
            dst_ref=parts_land.at[c, d],
            send_sem=parts_out.at[c, d],
            recv_sem=parts_in.at[c, d],
            device_id={"gy": ahead(place_y, d, lanes_y)},
            device_id_type=MESH,
        )
        for c in order
        for d in far_y
    }
    rim_copies = [
        pltpu.make_async_remote_copy(
            src_ref=rims,
            dst_ref=rims_land.at[side],
            send_sem=rims_out.at[side],
            recv_sem=rims_in.at[side],
            device_id={"gz": ahead(place_z, d, lanes_z)},
            device_id_type=MESH,
        )
        for side, d in ((0, 1), (1, lanes_z - 1))
    ]
    for c in order:
        if c == CLASSES:
            pack_rims(lanes_x, shift_z, cells_ref, sums_ref, packed[c])
        else:
            pack_class(lanes_x, shift_z, c, cells_ref, packed[c])
        if c == order[0]:
            pl.semaphore_wait(barrier, len(peers))
        for d in far_x:
            cell_copies[c, d].start()

    sub = lax.broadcasted_iota(jnp.int32, (BX, BZ), 0)
    lane = lax.broadcasted_iota(jnp.int32, (BX, BZ), 1)
    cell_x = place_x * BX + sub
    cells_y = lanes_y * BY
    starts_y = []
    for p in range(lanes_x):
        source = lax.rem(place_x - p + lanes_x, lanes_x)
        code = owner_ref[source, place_z, place_y]
        start_x, start_y, start_z = corner_of(start_ref, code, lanes_y, place_z)
        starts_y.append(start_y)
        shift_z = place_z * BZ - start_z
        rim_z = lane % RIM + jnp.where(lane < BZ // 2, -RIM, BZ) + shift_z
        along_x = profile(cell_x - start_x, PX)
        plane_ref[p, 0] = along_x * profile(lane + shift_z, PZ)
        plane_ref[p, 1] = along_x * profile(rim_z, PZ, lane % (BZ // 2) < RIM * CLASSES)
        row = lax.broadcasted_iota(jnp.int32, (cells_y, BZ), 0)
        along_y_ref[p] = profile(row - start_y, PY)

    weight_ref[...] = jnp.zeros(weight_ref.shape, jnp.float32)
    cell_y = place_y * BY + lax.broadcasted_iota(jnp.int32, (BY, BZ), 0)

    def weigh(code, carry):
        for step in (-1, 0, 1):
            layer = jnp.clip(place_z + step, 0, lanes_z - 1)
            start_x, start_y, start_z = corner_of(start_ref, code, lanes_y, layer)
            along = profile(cell_y - start_y, PY)
            plane = profile(cell_x - start_x, PX) * profile(
                place_z * BZ + lane - start_z, PZ, layer == place_z + step
            )
            for y in range(BY):
                weight_ref[y] = weight_ref[y] + plane * along[y : y + 1]
        return carry

    lax.fori_loop(0, lanes_x * lanes_y, weigh, 0)

    def blend(c):
        kind = 0 if c < CLASSES else 1
        for d in far_y + [0]:
            base = ahead(place_y, d, lanes_y) * BY

            def step(y, carry):
                row = base + y
                total = None
                for p in range(lanes_x):
                    q = jnp.clip(row - starts_y[p], 0, PY - 1)
                    held = packed[c] if p == 0 else cells_land[c]
                    if c < CLASSES:
                        cells = held[p, q].astype(jnp.float32)
                    else:
                        half = jnp.where(q >= FOLD, 1, 0)
                        cells = held[p, q - half * FOLD].astype(jnp.float32)
                        swapped = pltpu.roll(cells, BZ // 2, 1)
                        cells = jnp.where(lane // (BZ // 2) == half, cells, swapped)
                    term = cells * (plane_ref[p, kind] * along_y_ref[p, pl.ds(row, 1)])
                    total = term if total is None else total + term
                parts[c, d, y] = total
                return carry

            lax.fori_loop(0, BY, step, 0, unroll=2)
            if d:
                part_copies[c, d].start()

    def gathered(c, y):
        total = parts[c, 0, y]
        for d in range(1, lanes_y):
            total = total + parts_land[c, d, y]
        return total

    low_lanes = (lane < RIM) & (place_z > 0)
    high_lanes = (lane >= BZ - RIM) & (place_z < lanes_z - 1)

    def add_rims(y, carry):
        rims[y] = gathered(CLASSES, y)
        return carry

    def rim_of(c, y):
        low = pltpu.roll(rims_land[0, y], BZ // 2 - RIM * c, 1)
        high = pltpu.roll(rims_land[1, y], BZ - RIM - RIM * c, 1)
        return jnp.where(low_lanes, low, jnp.where(high_lanes, high, 0.0))

    def early(y, carry):
        weight_ref[y] = 1.0 / weight_ref[y]
        for c in range(CLASSES - 1):
            parts[c, 0, y] = (gathered(c, y) + rim_of(c, y)) * weight_ref[y]
        parts[CLASSES - 1, 0, y] = parts[CLASSES - 1, 0, y] + rim_of(CLASSES - 1, y)
        return carry

    def finish(y, carry):
        scores = [parts[c, 0, y] for c in range(CLASSES - 1)]
        scores.append(gathered(CLASSES - 1, y) * weight_ref[y])
        top = functools.reduce(jnp.maximum, scores)
        powers = [jnp.exp(s - top) for s in scores]
        norm = 1.0 / functools.reduce(jnp.add, powers)
        for c in range(CLASSES):
            out_ref[y, c] = powers[c] * norm
        return carry

    for c in order:
        for d in far_x:
            cell_copies[c, d].wait_recv()
        blend(c)
        if c == 1:
            for d in far_y:
                part_copies[CLASSES, d].wait_recv()
            lax.fori_loop(0, BY, add_rims, 0, unroll=4)
            for copy in rim_copies:
                copy.start()

    for copy in rim_copies:
        copy.wait_recv()
    for c in range(CLASSES - 1):
        for d in far_y:
            part_copies[c, d].wait_recv()
    lax.fori_loop(0, BY, early, 0, unroll=4)
    for d in far_y:
        part_copies[CLASSES - 1, d].wait_recv()
    lax.fori_loop(0, BY, finish, 0, unroll=8)
    for copy in list(cell_copies.values()) + list(part_copies.values()) + rim_copies:
        copy.wait_send()


VMEM = pl.BlockSpec(memory_space=pltpu.VMEM)
SMEM = pl.BlockSpec(memory_space=pltpu.SMEM)


def per_device(patch_logits, patch_start, patch_owner):
    lanes_x = lax.axis_size("gx")
    lanes_y = lax.axis_size("gy")
    lanes_z = lax.axis_size("gz")
    row_shapes = [(lanes_x, PY, BX, BZ)] * CLASSES + [(lanes_x, FOLD, BX, BZ)]
    parts_shape = (ROWS, lanes_y, BY, BX, BZ)
    probs = pl.pallas_call(
        functools.partial(blend_kernel, lanes_x, lanes_y, lanes_z),
        out_shape=jax.ShapeDtypeStruct((BY, CLASSES, BX, BZ), jnp.float32),
        in_specs=[SMEM, SMEM, VMEM],
        out_specs=VMEM,
        scratch_shapes=[
            pltpu.VMEM((lanes_x, lanes_y * BY, BZ), jnp.float32),
            pltpu.VMEM((lanes_x, 2, BX, BZ), jnp.float32),
            pltpu.VMEM((BY, BX, BZ), jnp.float32),
            pltpu.VMEM((lanes_x * BX, PY * CLASSES * PZ), jnp.bfloat16),
            pltpu.VMEM((FOLD, lanes_x * BX, BZ), jnp.float32),
            *[pltpu.VMEM(shape, jnp.bfloat16) for shape in row_shapes * 2],
            pltpu.VMEM(parts_shape, jnp.float32),
            pltpu.VMEM(parts_shape, jnp.float32),
            pltpu.VMEM((BY, BX, BZ), jnp.float32),
            pltpu.VMEM((2, BY, BX, BZ), jnp.float32),
            pltpu.SemaphoreType.DMA((ROWS, lanes_x)),
            pltpu.SemaphoreType.DMA((ROWS, lanes_x)),
            pltpu.SemaphoreType.DMA((ROWS, lanes_y)),
            pltpu.SemaphoreType.DMA((ROWS, lanes_y)),
            pltpu.SemaphoreType.DMA((2,)),
            pltpu.SemaphoreType.DMA((2,)),
        ],
        compiler_params=pltpu.CompilerParams(collective_id=0, has_side_effects=True),
    )(
        jnp.transpose(patch_start, (0, 3, 2, 1)),
        jnp.transpose(patch_owner, (0, 2, 1)),
        patch_logits[0, 0, 0],
    )
    return jnp.transpose(probs, (2, 0, 1, 3))


def solution(mesh):
    return jax.shard_map(
        per_device,
        mesh=mesh,
        in_specs=(P("gx", "gy", "gz", None, None), P(), P()),
        out_specs=P("gx", "gy", None, "gz"),
        check_vma=False,
    )
```

profile of v0, /device:TPU:0, one launch (start us, length us, event | category | flops | bytes accessed | tf_op | source)
XLA Modules:
  0.0 50.2 jit_solution(4214785034421236385)
XLA Ops:
  0.0 48.3 %shard_map.37 = f32[32,3,8,128]{3,2,1,0:T(8,128)} custom-call(s32[4,3,2,4]{3,2,1,0:T(2,128)} %bitcast.6, s32[4,2,4]{2,1,0:T(2,128)} %bitcast.7, bf16[24,20736]{1,0:T(8,128)(2,1)} %bitcast.5), custom_call_target="tpu_custom_call" | custom-call | tf_op jit(solution)/shard_map/pallas_call | solution.py:306
  48.3 1.8 %copy.4 = f32[8,32,3,128]{3,1,2,0:T(8,128)} copy(f32[8,32,3,128]{3,0,2,1:T(8,128)} %bitcast.4) | data formatting | bytes 786432 | tf_op jit(solution)/shard_map/transpose | solution.py:335
where the time goes:
time: 50.4 us; the launch traced here: 50.2 us
  Pallas kernels  48.3 us (96%)
  local copies, waits for them, and re-layouts  1.82 us (4%)
    pallas_call x1, Pallas kernels, per_device(): pl.pallas_call(functools.partial(blend_kernel, lanes_x, lanes_y, lanes_z)...  48.3 us
    transpose x1, local copies, waits for them, and re-layouts, per_device(): return jnp.transpose(probs, (2, 0, 1, 3))  1.82 us

commit v1 on v0

v1 whole, which is shorter than its diff:
```python
import functools

import jax
import jax.numpy as jnp
from jax import lax
from jax.experimental import pallas as pl
from jax.experimental.pallas import tpu as pltpu
from jax.sharding import PartitionSpec as P

CLASSES = 3
BX = 8
BY = 32
BZ = 128
PX = 24
PY = 48
PZ = 144
RIM = PZ - BZ
STEP = 8
TILES = PX // BX
LINES = PY // STEP
ROWS = BY // STEP
MAIN = LINES * CLASSES
DIFFS = CLASSES - 1
SLOTS = BZ // RIM
SPAN = SLOTS * STEP
GROUP = STEP * CLASSES * PZ
PHASES = BZ // RIM
Y_FIRST = 4
X_FIRST = STEP - Y_FIRST
MESH = pl.DeviceIdType.MESH
F32 = jnp.float32
BF16 = jnp.bfloat16


def profile(offsets, length, keep=True):
    inside = (offsets >= 0) & (offsets < length) & keep
    centre = (length - 1) / 2.0
    spread = length / 4.0
    values = jnp.exp((offsets.astype(F32) - centre) ** 2 * (-0.5 / (spread * spread)))
    return jnp.where(inside, values, 0.0)


def blend_kernel(
    lanes_x, lanes_y, lanes_z,
    start_ref, owner_ref, logits_ref, out_ref,
    raw_ref, cells_ref, move_ref, packed, rim_land, parts, parts_land,
    rows, rows_land, edge_land, sums, sums_land,
    along_ref, plane_ref, rim_plane_ref, row_along_ref, row_plane_ref, edge_plane_ref, weight_ref,
    raw_in, cells_out, cells_in, rims_out, rims_in, parts_out, parts_in,
    rows_out, rows_in, edges_out, edges_in, sums_out, sums_in,
    *land,
):
    place_x = lax.axis_index("gx")
    place_y = lax.axis_index("gy")
    place_z = lax.axis_index("gz")
    sides = (1,) if lanes_z == 2 else (1, lanes_z - 1)
    cells_y = lanes_y * BY

    def ahead(place, d, size):
        return lax.rem(place + d, size)

    def corner_of(code, layer):
        return [start_ref[code // lanes_y, k, layer, lax.rem(code, lanes_y)] for k in range(3)]

    def settle(ref, sem):
        pltpu.make_async_copy(ref, ref, sem).wait()

    barrier = pltpu.get_barrier_semaphore()
    peers = [{"gz": ahead(place_z, s, lanes_z)} for s in sides]
    for axis, place, size in (("gx", place_x, lanes_x), ("gy", place_y, lanes_y)):
        for d in range(1, size):
            there = {axis: ahead(place, d, size)}
            peers.append(there)
            peers += [{**there, "gz": ahead(place_z, s, lanes_z)} for s in sides]
    for peer in peers:
        pl.semaphore_signal(barrier, inc=1, device_id=peer, device_id_type=MESH)

    groups = PY // STEP
    loads = []
    for g in range(groups):
        lanes = pl.ds(g * GROUP, GROUP)
        loads.append(pltpu.make_async_copy(logits_ref.at[:, lanes], raw_ref.at[:, lanes], raw_in.at[g]))
        loads[-1].start()

    code = owner_ref[place_x, place_z, place_y]
    start_x, start_y, start_z = corner_of(code, place_z)
    shift_z = place_z * BZ - start_z

    k = lax.broadcasted_iota(jnp.int32, (2 * BZ, 2 * BZ), 0)
    n = lax.broadcasted_iota(jnp.int32, (2 * BZ, 2 * BZ), 1)
    edge = lax.rem(n, RIM) + shift_z
    edge = edge + jnp.where(edge < RIM, BZ, -RIM)
    ahead_by = k - jnp.where(n < BZ, n + shift_z, edge)
    for m in range(PHASES):
        move_ref[m] = jnp.where(ahead_by == m * RIM, 1.0, 0.0).astype(BF16)

    r = lax.broadcasted_iota(jnp.int32, (PX, PX), 0)
    p = lax.broadcasted_iota(jnp.int32, (PX, PX), 1) + lax.rem(start_x, PX)
    pick = jnp.where(jnp.where(p >= PX, p - PX, p) == r, 1.0, 0.0).astype(BF16)
    for g in range(groups):
        lanes = slice(g * GROUP, (g + 1) * GROUP)
        loads[g].wait()
        cells = jnp.dot(pick, raw_ref[:, lanes], preferred_element_type=F32)
        cells = cells.astype(BF16)
        for i in range(GROUP // BZ):
            cells_ref[g * (GROUP // BZ) + i] = cells[:, i * BZ : (i + 1) * BZ]

    lane = lax.broadcasted_iota(jnp.int32, (BX, BZ), 1)
    sub = lax.broadcasted_iota(jnp.int32, (BX, BZ), 0)
    slot_of_lane = lane // RIM

    def line_of(y, y0):
        return jnp.clip(lax.shift_right_arithmetic(y - y0, 3), 0, LINES - 1)

    def pack(r):
        phase = lax.rem(r - start_y + cells_y, STEP)
        first = (start_y + phase) // STEP
        for c in range(CLASSES):
            at = phase * (STEP * CLASSES + CLASSES) + c * (STEP + 1)
            block = at // PHASES
            halves = []
            for half in range(2):
                lines = [cells_ref[u * (GROUP // BZ) + block + half] for u in range(LINES)]
                halves.append(jnp.concatenate(lines, axis=0))
            moved = jnp.dot(
                jnp.concatenate(halves, axis=1), move_ref[lax.rem(at, PHASES)], preferred_element_type=F32
            )
            rims = [jnp.zeros((BX, BZ), F32)] * TILES
            for u in range(LINES):
                here = slot_of_lane == lax.rem(first + u, SLOTS)
                for j in range(TILES):
                    cells = slice(u * PX + j * BX, u * PX + (j + 1) * BX)
                    packed[r, j, u * CLASSES + c] = moved[cells, :BZ].astype(BF16)
                    rims[j] = jnp.where(here, moved[cells, BZ:], rims[j])
            for j in range(TILES):
                packed[r, j, MAIN + c] = rims[j].astype(BF16)

    def cut_rows(k):
        for b in range(lanes_y):
            for t in range(ROWS):
                at = line_of(b * BY + t * STEP + k, start_y) * CLASSES
                for j in range(TILES):
                    for c in range(CLASSES):
                        rows[k, b, j, t * CLASSES + c] = packed[k, j, at + c]

    far_x = sorted(range(1, lanes_x), key=lambda d: -min(d, lanes_x - d))
    far_y = sorted(range(1, lanes_y), key=lambda d: -min(d, lanes_y - d))

    def remote(src, dst, send, recv, where):
        pltpu.make_async_remote_copy(
            src_ref=src, dst_ref=dst, send_sem=send, recv_sem=recv, device_id=where, device_id_type=MESH
        ).start()

    def send_x(k):
        r = Y_FIRST + k
        for d in far_x + [0]:
            there = ahead(place_x, d, lanes_x)
            tile = lax.rem(there, TILES)
            if d:
                cells = packed.at[r, tile, pl.ds(0, MAIN)]
                remote(cells, land[k].at[d], cells_out.at[k], cells_in.at[k], {"gx": there})
            rims = packed.at[r, tile, pl.ds(MAIN, CLASSES)]
            for s, step in enumerate(sides):
                where = {"gx": there, "gz": ahead(place_z, step, lanes_z)}
                remote(rims, rim_land.at[k, s, d], rims_out.at[k], rims_in.at[k], where)

    def send_y(k):
        for d in far_y + [0]:
            there = ahead(place_y, d, lanes_y)
            if d:
                remote(rows.at[k, there], rows_land.at[k, d], rows_out.at[k], rows_in.at[k], {"gy": there})
            rims = packed.at[k, pl.ds(0, TILES), pl.ds(MAIN, CLASSES)]
            for s, step in enumerate(sides):
                where = {"gy": there, "gz": ahead(place_z, step, lanes_z)}
                remote(rims, edge_land.at[k, s, d], edges_out.at[k], edges_in.at[k], where)

    for k in range(max(X_FIRST, Y_FIRST)):
        if k < Y_FIRST:
            pack(k)
            cut_rows(k)
            if k == 0:
                pl.semaphore_wait(barrier, len(peers))
            send_y(k)
        if k < X_FIRST:
            pack(Y_FIRST + k)
            if k == 0 and not Y_FIRST:
                pl.semaphore_wait(barrier, len(peers))
            send_x(k)

    cell_x = place_x * BX + sub
    cell_z = place_z * BZ + lane
    row = lax.broadcasted_iota(jnp.int32, (cells_y, BZ), 0)
    cell_y = place_y * BY + lax.broadcasted_iota(jnp.int32, (BY, BZ), 0)
    low = [place_z > 0 if lanes_z == 2 else step == 1 for step in sides]
    layers = [place_z + jnp.where(side, -1, 1) for side in low]
    kept = [jnp.clip(layer, 0, lanes_z - 1) for layer in layers]
    rim_z = [place_z * BZ + lax.rem(lane, RIM) + jnp.where(side, 0, BZ - RIM) for side in low]

    starts_y = []
    rim_starts_y = {}
    for d in range(lanes_x):
        source = lax.rem(place_x - d + lanes_x, lanes_x)
        x0, y0, z0 = corner_of(owner_ref[source, place_z, place_y], place_z)
        starts_y.append(y0)
        plane_ref[d] = profile(cell_x - x0, PX) * profile(cell_z - z0, PZ)
        along_ref[d] = profile(row - y0, PY)
        for s, layer in enumerate(layers):
            x0, y0, z0 = corner_of(owner_ref[source, kept[s], place_y], kept[s])
            rim_starts_y[s, d] = y0
            rim_plane_ref[s, d] = profile(cell_x - x0, PX) * profile(rim_z[s] - z0, PZ, layer == kept[s])
    edge_starts_y = {}
    for d in range(lanes_y):
        source = lax.rem(place_y - d + lanes_y, lanes_y)
        x0, y0, z0 = corner_of(owner_ref[place_x, place_z, source], place_z)
        row_along_ref[d] = profile(cell_y - y0, PY)
        along_z = profile(cell_z - z0, PZ)
        for b in range(lanes_x):
            row_plane_ref[d, b] = profile(b * BX + sub - x0, PX) * along_z
        for s, layer in enumerate(layers):
            x0, y0, z0 = corner_of(owner_ref[place_x, kept[s], source], kept[s])
            edge_starts_y[s, d] = y0
            along_z = profile(rim_z[s] - z0, PZ, layer == kept[s])
            for b in range(lanes_x):
                edge_plane_ref[s, d, b] = profile(b * BX + sub - x0, PX) * along_z

    def weigh(code, carry):
        for step in (0, 1) if lanes_z == 2 else (-1, 0, 1):
            reach = step if lanes_z == 2 else place_z + step
            layer = jnp.clip(reach, 0, lanes_z - 1)
            x0, y0, z0 = corner_of(code, layer)
            along = profile(cell_y - y0, PY)
            plane = profile(cell_x - x0, PX) * profile(cell_z - z0, PZ, layer == reach)
            for y in range(BY):
                weight_ref[y] = weight_ref[y] + plane * along[y : y + 1]
        return carry

    weight_ref[...] = jnp.zeros(weight_ref.shape, F32)
    lax.fori_loop(0, lanes_x * lanes_y, weigh, 0)
    for y in range(BY):
        weight_ref[y] = 1.0 / weight_ref[y]

    spans = -(-cells_y // SPAN)
    rim_lane = [jnp.where(side, lane, BZ - 1 - lane) < RIM for side in low]

    def blend_x(k):
        r = Y_FIRST + k
        settle(land[k].at[pl.ds(1, lanes_x - 1)], cells_in.at[k])
        settle(rim_land.at[k], rims_in.at[k])
        rims = {}
        for s in range(len(sides)):
            for d in range(lanes_x):
                cells = [rim_land[k, s, d, c].astype(F32) for c in range(CLASSES)]
                for span in range(spans):
                    y = span * SPAN + slot_of_lane * STEP + r
                    weight = rim_plane_ref[s, d] * profile(y - rim_starts_y[s, d], PY)
                    for e in range(DIFFS):
                        term = (cells[e + 1] - cells[0]) * weight
                        rims[s, span, e] = rims[s, span, e] + term if d else term
            for span in range(spans):
                for e in range(DIFFS):
                    total = rims[s, span, e]
                    rims[s, span, e] = jnp.where(low[s], total, pltpu.roll(total, BZ - RIM, 1))
        for b in range(lanes_y):
            for t in range(ROWS):
                y = b * BY + t * STEP + r
                slot = (b * ROWS + t) % SLOTS
                totals = []
                for e in range(DIFFS):
                    total = 0.0
                    for s in range(len(sides)):
                        rim = rims[s, b * BY // SPAN, e]
                        rim = pltpu.roll(rim, BZ - slot * RIM, 1) if slot else rim
                        total = jnp.where(rim_lane[s], rim, total)
                    totals.append(total)
                for d in range(lanes_x):
                    at = line_of(y, starts_y[d]) * CLASSES
                    if d:
                        cells = [land[k][d, at + c].astype(F32) for c in range(CLASSES)]
                    else:
                        tile = lax.rem(place_x, TILES)
                        cells = [packed[r, tile, at + c].astype(F32) for c in range(CLASSES)]
                    weight = plane_ref[d] * along_ref[d, pl.ds(y, 1)]
                    for e in range(DIFFS):
                        totals[e] = totals[e] + (cells[e + 1] - cells[0]) * weight
                for e in range(DIFFS):
                    parts[k, b, t, e] = totals[e]
        for d in far_y:
            there = ahead(place_y, d, lanes_y)
            remote(parts.at[k, there], parts_land.at[k, d], parts_out.at[k], parts_in.at[k], {"gy": there})

    def blend_y(k):
        settle(rows_land.at[k, pl.ds(1, lanes_y - 1)], rows_in.at[k])
        settle(edge_land.at[k], edges_in.at[k])
        first = lax.rem(place_y * ROWS, SLOTS)
        rims = {}
        for s in range(len(sides)):
            for d in range(lanes_y):
                y = (place_y * ROWS - first + slot_of_lane) * STEP + k
                along = profile(y - edge_starts_y[s, d], PY)
                for j in range(min(TILES, lanes_x)):
                    cells = [edge_land[k, s, d, j, c].astype(F32) for c in range(CLASSES)]
                    terms = [(cells[e + 1] - cells[0]) * along for e in range(DIFFS)]
                    for b in range(j, lanes_x, TILES):
                        for e in range(DIFFS):
                            term = terms[e] * edge_plane_ref[s, d, b]
                            rims[s, b, e] = rims[s, b, e] + term if d else term
        turn = [lax.rem(2 * BZ - first * RIM - jnp.where(side, 0, RIM), BZ) for side in low]
        rims = {at: pltpu.roll(total, turn[at[0]], 1) for at, total in rims.items()}
        for j in range(min(TILES, lanes_x)):
            for t in range(ROWS):
                y = t * STEP + k
                totals = {}
                for b in range(j, lanes_x, TILES):
                    for e in range(DIFFS):
                        total = 0.0
                        for s in range(len(sides)):
                            rim = pltpu.roll(rims[s, b, e], BZ - t * RIM, 1) if t else rims[s, b, e]
                            total = jnp.where(rim_lane[s], rim, total)
                        totals[b, e] = total
                for d in range(lanes_y):
                    if d:
                        cells = [rows_land[k, d, j, t * CLASSES + c].astype(F32) for c in range(CLASSES)]
                    else:
                        cells = [rows[k, place_y, j, t * CLASSES + c].astype(F32) for c in range(CLASSES)]
                    along = row_along_ref[d, pl.ds(y, 1)]
                    terms = [(cells[e + 1] - cells[0]) * along for e in range(DIFFS)]
                    for b in range(j, lanes_x, TILES):
                        for e in range(DIFFS):
                            totals[b, e] = totals[b, e] + terms[e] * row_plane_ref[d, b]
                for (b, e), total in totals.items():
                    sums[k, b, t, e] = total
        hop(0, k)

    def take(k, way, b):
        settle(sums_land.at[k, way, b], sums_in.at[k, way, b])
        for t in range(ROWS):
            for e in range(DIFFS):
                sums[k, b, t, e] = sums[k, b, t, e] + sums_land[k, way, b, t, e]

    def hop(h, k):
        for way in range(2):
            @pl.when(place_x == (lanes_x - 1 - h if way else h))
            def _():
                past = range(lanes_x - 1 - h) if way else range(lanes_x - 1, h, -1)
                there = place_x - 1 if way else place_x + 1
                for b in past:
                    if h:
                        take(k, way, b)
                    remote(
                        sums.at[k, b], sums_land.at[k, way, b], sums_out.at[k], sums_in.at[k, way, b], {"gx": there}
                    )

    def write(y, totals):
        scores = [total * weight_ref[y] for total in totals]
        top = jnp.maximum(functools.reduce(jnp.maximum, scores), 0.0)
        powers = [jnp.exp(-top)] + [jnp.exp(s - top) for s in scores]
        norm = 1.0 / functools.reduce(jnp.add, powers)
        for c in range(CLASSES):
            out_ref[y, c] = powers[c] * norm

    def finish_x(k):
        settle(parts_land.at[k, pl.ds(1, lanes_y - 1)], parts_in.at[k])
        for t in range(ROWS):
            totals = []
            for e in range(DIFFS):
                total = parts[k, place_y, t, e]
                for d in far_y:
                    total = total + parts_land[k, d, t, e]
                totals.append(total)
            write(t * STEP + Y_FIRST + k, totals)

    def finish_y(k):
        @pl.when(place_x > 0)
        def _():
            take(k, 0, place_x)

        @pl.when(place_x < lanes_x - 1)
        def _():
            take(k, 1, place_x)

        for t in range(ROWS):
            write(t * STEP + k, [sums[k, place_x, t, e] for e in range(DIFFS)])

    for i in range(max(X_FIRST, Y_FIRST) + lanes_x):
        if i < Y_FIRST:
            blend_y(i)
        if i < X_FIRST:
            blend_x(i)
        for h in range(1, lanes_x - 1):
            if 0 <= i - h + 1 < Y_FIRST:
                hop(h, i - h + 1)
        if 0 <= i - 1 < X_FIRST:
            finish_x(i - 1)
        if 0 <= i - lanes_x + 2 < Y_FIRST:
            finish_y(i - lanes_x + 2)

    for k in range(X_FIRST):
        settle(land[k].at[pl.ds(1, lanes_x - 1)], cells_out.at[k])
        settle(rim_land.at[k], rims_out.at[k])
        settle(parts_land.at[k, pl.ds(1, lanes_y - 1)], parts_out.at[k])
    for k in range(Y_FIRST):
        settle(rows_land.at[k, pl.ds(1, lanes_y - 1)], rows_out.at[k])
        settle(edge_land.at[k], edges_out.at[k])
        settle(sums.at[k, pl.ds(0, lanes_x - 1)], sums_out.at[k])


VMEM = pl.BlockSpec(memory_space=pltpu.VMEM)
SMEM = pl.BlockSpec(memory_space=pltpu.SMEM)


def per_device(patch_logits, patch_start, patch_owner):
    lanes_x = lax.axis_size("gx")
    lanes_y = lax.axis_size("gy")
    lanes_z = lax.axis_size("gz")
    sides = 1 if lanes_z == 2 else 2
    lines = PY * CLASSES * PZ
    dma = pltpu.SemaphoreType.DMA
    probs = pl.pallas_call(
        functools.partial(blend_kernel, lanes_x, lanes_y, lanes_z),
        out_shape=pltpu.VMEM((BY, CLASSES, BX, BZ), F32),
        in_specs=[SMEM, SMEM, pl.BlockSpec(memory_space=pl.ANY)],
        out_specs=VMEM,
        scratch_shapes=[
            pltpu.VMEM((PX, lines), BF16),
            pltpu.VMEM((lines // BZ, PX, BZ), BF16),
            pltpu.VMEM((PHASES, 2 * BZ, 2 * BZ), BF16),
            pltpu.VMEM((STEP, TILES, MAIN + CLASSES, BX, BZ), BF16),
            pltpu.VMEM((X_FIRST, sides, lanes_x, CLASSES, BX, BZ), BF16),
            pltpu.VMEM((X_FIRST, lanes_y, ROWS, DIFFS, BX, BZ), F32),
            pltpu.VMEM((X_FIRST, lanes_y, ROWS, DIFFS, BX, BZ), F32),
            pltpu.VMEM((Y_FIRST, lanes_y, TILES, ROWS * CLASSES, BX, BZ), BF16),
            pltpu.VMEM((Y_FIRST, lanes_y, TILES, ROWS * CLASSES, BX, BZ), BF16),
            pltpu.VMEM((Y_FIRST, sides, lanes_y, TILES, CLASSES, BX, BZ), BF16),
            pltpu.VMEM((Y_FIRST, lanes_x, ROWS, DIFFS, BX, BZ), F32),
            pltpu.VMEM((Y_FIRST, 2, lanes_x, ROWS, DIFFS, BX, BZ), F32),
            pltpu.VMEM((lanes_x, lanes_y * BY, BZ), F32),
            pltpu.VMEM((lanes_x, BX, BZ), F32),
            pltpu.VMEM((sides, lanes_x, BX, BZ), F32),
            pltpu.VMEM((lanes_y, BY, BZ), F32),
            pltpu.VMEM((lanes_y, lanes_x, BX, BZ), F32),
            pltpu.VMEM((sides, lanes_y, lanes_x, BX, BZ), F32),
            pltpu.VMEM((BY, BX, BZ), F32),
            dma((PY // STEP,)),
            *[dma((X_FIRST,))] * 6,
            *[dma((Y_FIRST,))] * 5,
            dma((Y_FIRST, 2, lanes_x)),
            *[pltpu.VMEM((lanes_x, MAIN, BX, BZ), BF16)] * X_FIRST,
        ],
        compiler_params=pltpu.CompilerParams(collective_id=0, has_side_effects=True),
    )(
        jnp.transpose(patch_start, (0, 3, 2, 1)),
        jnp.transpose(patch_owner, (0, 2, 1)),
        patch_logits[0, 0, 0],
    )
    return jnp.transpose(probs, (2, 0, 1, 3))


def solution(mesh):
    return jax.shard_map(
        per_device,
        mesh=mesh,
        in_specs=(P("gx", "gy", "gz", None, None), P(), P()),
        out_specs=P("gx", "gy", None, "gz"),
        check_vma=False,
    )
```

time: 50.4 us -> 39.1 us (0.78)
  Pallas kernels: 48.3 us -> 38 us
  local copies, waits for them, and re-layouts: 1.82 us -> 0.82 us
    pallas_call x1, Pallas kernels: 48.3 us -> 38 us  [per_device(): pl.pallas_call(functools.partial(blend_kernel, lanes_x, lanes_y, lanes_z)...]
    transpose x1, local copies, waits for them, and re-layouts: 1.82 us -> 0.82 us  [per_device(): return jnp.transpose(probs, (2, 0, 1, 3))]
where the time goes in v1:
time: 39.1 us; the launch traced here: 38.9 us
  Pallas kernels  38 us (97%)
  local copies, waits for them, and re-layouts  0.82 us (2%)
    pallas_call x1, Pallas kernels, per_device(): pl.pallas_call(functools.partial(blend_kernel, lanes_x, lanes_y, lanes_z)...  38 us
    transpose x1, local copies, waits for them, and re-layouts, per_device(): return jnp.transpose(probs, (2, 0, 1, 3))  0.82 us

profile of v1, /device:TPU:0, one launch (start us, length us, event | category | flops | bytes accessed | tf_op | source)
XLA Modules:
  0.0 38.9 jit_solution(3529042707990245084)
XLA Ops:
  0.0 38.0 %shard_map.37 = f32[32,3,8,128]{3,2,1,0:T(8,128)S(1)} custom-call(s32[4,3,2,4]{3,2,1,0:T(2,128)} %bitcast.6, s32[4,2,4]{2,1,0:T(2,128)} %bitcast.7, bf16[24,20736]{1,0:T(8,128)(2,1)} %bitcast.5), custom_call_target="tpu_custom_call" | custom-call | tf_op jit(solution)/shard_map/pallas_call | solution.py:418
  38.1 0.8 %copy.4 = f32[8,32,3,128]{3,1,2,0:T(8,128)} copy(f32[8,32,3,128]{3,0,2,1:T(8,128)S(1)} %bitcast.4) | data formatting | bytes 786432 | tf_op jit(solution)/shard_map/transpose | solution.py:455

commit v2 on v1

--- a/solution.py
+++ b/solution.py
@@ -27,6 +27,7 @@
 PHASES = BZ // RIM
 Y_FIRST = 4
 X_FIRST = STEP - Y_FIRST
+AHEAD = 2
 MESH = pl.DeviceIdType.MESH
 F32 = jnp.float32
 BF16 = jnp.bfloat16
@@ -40,14 +41,23 @@
     return jnp.where(inside, values, 0.0)
 
 
+def events(send_x, blend_y, blend_x, join_y, cross_x, finish_x, finish_y):
+    return [
+        (blend_y, 0), (blend_x, 0), (blend_y, 1), (blend_y, 2), (join_y, 0), (send_x, 2), (blend_x, 1),
+        (blend_y, 3), (finish_x, 0), (join_y, 1), (send_x, 3), (cross_x, 0), (join_y, 2), (finish_x, 1), (blend_x, 2),
+        (cross_x, 1), (finish_y, 0), (join_y, 3), (cross_x, 2), (finish_y, 1), (blend_x, 3), (cross_x, 3),
+        (finish_x, 2), (finish_y, 2), (finish_x, 3), (finish_y, 3),
+    ]
+
+
 def blend_kernel(
     lanes_x, lanes_y, lanes_z,
-    start_ref, owner_ref, logits_ref, out_ref,
-    raw_ref, cells_ref, move_ref, packed, rim_land, parts, parts_land,
-    rows, rows_land, edge_land, sums, sums_land,
+    starts_ref, owners_ref, logits_ref, out_ref,
+    start_ref, owner_ref, raw_ref, cells_ref, move_ref, packed, rim_land, parts, parts_land,
+    rows, rows_land, edge_land, sums, halves, halves_land, pair_land, cross_land,
     along_ref, plane_ref, rim_plane_ref, row_along_ref, row_plane_ref, edge_plane_ref, weight_ref,
-    raw_in, cells_out, cells_in, rims_out, rims_in, parts_out, parts_in,
-    rows_out, rows_in, edges_out, edges_in, sums_out, sums_in,
+    table_in, raw_in, cells_out, cells_in, rims_out, rims_in, parts_out, parts_in,
+    rows_out, rows_in, edges_out, edges_in, halves_out, halves_in, pair_out, pair_in, cross_out, cross_in,
     *land,
 ):
     place_x = lax.axis_index("gx")
@@ -65,13 +75,22 @@
     def settle(ref, sem):
         pltpu.make_async_copy(ref, ref, sem).wait()
 
+    side_y = lax.rem(place_y, 2)
+    next_y = place_y + 1 - 2 * side_y
+    same_y = [lax.rem(place_y + 2 * o, lanes_y) for o in range(lanes_y // 2)]
+    side_x = lax.rem(place_x, 2)
+    pair_x = place_x // 2
+    tables = [
+        pltpu.make_async_copy(starts_ref, start_ref, table_in.at[0]),
+        pltpu.make_async_copy(owners_ref, owner_ref, table_in.at[1]),
+    ]
+    for table in tables:
+        table.start()
     barrier = pltpu.get_barrier_semaphore()
-    peers = [{"gz": ahead(place_z, s, lanes_z)} for s in sides]
-    for axis, place, size in (("gx", place_x, lanes_x), ("gy", place_y, lanes_y)):
-        for d in range(1, size):
-            there = {axis: ahead(place, d, size)}
-            peers.append(there)
-            peers += [{**there, "gz": ahead(place_z, s, lanes_z)} for s in sides]
+    near = [{"gx": ahead(place_x, d, lanes_x)} for d in range(1, lanes_x)]
+    peers = near + [{"gy": ahead(place_y, d, lanes_y)} for d in range(1, lanes_y)]
+    for there in near + [{}, {"gy": next_y}]:
+        peers += [{**there, "gz": ahead(place_z, s, lanes_z)} for s in sides]
     for peer in peers:
         pl.semaphore_signal(barrier, inc=1, device_id=peer, device_id_type=MESH)
 
@@ -82,6 +101,8 @@
         loads.append(pltpu.make_async_copy(logits_ref.at[:, lanes], raw_ref.at[:, lanes], raw_in.at[g]))
         loads[-1].start()
 
+    for table in tables:
+        table.wait()
     code = owner_ref[place_x, place_z, place_y]
     start_x, start_y, start_z = corner_of(code, place_z)
     shift_z = place_z * BZ - start_z
@@ -136,12 +157,16 @@
                 packed[r, j, MAIN + c] = rims[j].astype(BF16)
 
     def cut_rows(k):
-        for b in range(lanes_y):
+        for q in range(2):
             for t in range(ROWS):
-                at = line_of(b * BY + t * STEP + k, start_y) * CLASSES
+                line = lax.shift_right_arithmetic(q * BY + t * STEP + k - start_y, 3)
+                for b in range(q + 2, lanes_y, 2):
+                    other = lax.shift_right_arithmetic(b * BY + t * STEP + k - start_y, 3)
+                    line = jnp.where((other >= 0) & (other < LINES), other, line)
+                at = jnp.clip(line, 0, LINES - 1) * CLASSES
                 for j in range(TILES):
                     for c in range(CLASSES):
-                        rows[k, b, j, t * CLASSES + c] = packed[k, j, at + c]
+                        rows[k, q, j, t * CLASSES + c] = packed[k, j, at + c]
 
     far_x = sorted(range(1, lanes_x), key=lambda d: -min(d, lanes_x - d))
     far_y = sorted(range(1, lanes_y), key=lambda d: -min(d, lanes_y - d))
@@ -165,13 +190,11 @@
                 remote(rims, rim_land.at[k, s, d], rims_out.at[k], rims_in.at[k], where)
 
     def send_y(k):
-        for d in far_y + [0]:
-            there = ahead(place_y, d, lanes_y)
-            if d:
-                remote(rows.at[k, there], rows_land.at[k, d], rows_out.at[k], rows_in.at[k], {"gy": there})
-            rims = packed.at[k, pl.ds(0, TILES), pl.ds(MAIN, CLASSES)]
-            for s, step in enumerate(sides):
-                where = {"gy": there, "gz": ahead(place_z, step, lanes_z)}
+        remote(rows.at[k, 1 - side_y], rows_land.at[k], rows_out.at[k], rows_in.at[k], {"gy": next_y})
+        rims = packed.at[k, pl.ds(0, TILES), pl.ds(MAIN, CLASSES)]
+        for s, step in enumerate(sides):
+            for d, there in enumerate(({}, {"gy": next_y})):
+                where = {**there, "gz": ahead(place_z, step, lanes_z)}
                 remote(rims, edge_land.at[k, s, d], edges_out.at[k], edges_in.at[k], where)
 
     for k in range(max(X_FIRST, Y_FIRST)):
@@ -185,7 +208,8 @@
             pack(Y_FIRST + k)
             if k == 0 and not Y_FIRST:
                 pl.semaphore_wait(barrier, len(peers))
-            send_x(k)
+            if k < AHEAD:
+                send_x(k)
 
     cell_x = place_x * BX + sub
     cell_z = place_z * BZ + lane
@@ -209,10 +233,10 @@
             rim_starts_y[s, d] = y0
             rim_plane_ref[s, d] = profile(cell_x - x0, PX) * profile(rim_z[s] - z0, PZ, layer == kept[s])
     edge_starts_y = {}
-    for d in range(lanes_y):
-        source = lax.rem(place_y - d + lanes_y, lanes_y)
+    for d, source in enumerate((place_y, next_y)):
         x0, y0, z0 = corner_of(owner_ref[place_x, place_z, source], place_z)
-        row_along_ref[d] = profile(cell_y - y0, PY)
+        for o, b in enumerate(same_y):
+            row_along_ref[o, d] = profile((b - place_y) * BY + cell_y - y0, PY)
         along_z = profile(cell_z - z0, PZ)
         for b in range(lanes_x):
             row_plane_ref[d, b] = profile(b * BX + sub - x0, PX) * along_z
@@ -289,65 +313,86 @@
             remote(parts.at[k, there], parts_land.at[k, d], parts_out.at[k], parts_in.at[k], {"gy": there})
 
     def blend_y(k):
-        settle(rows_land.at[k, pl.ds(1, lanes_y - 1)], rows_in.at[k])
+        settle(rows_land.at[k], rows_in.at[k])
         settle(edge_land.at[k], edges_in.at[k])
         first = lax.rem(place_y * ROWS, SLOTS)
         rims = {}
         for s in range(len(sides)):
-            for d in range(lanes_y):
-                y = (place_y * ROWS - first + slot_of_lane) * STEP + k
-                along = profile(y - edge_starts_y[s, d], PY)
+            for d in range(2):
+                along = []
+                for b in same_y:
+                    y = (b * ROWS - first + slot_of_lane) * STEP + k
+                    along.append(profile(y - edge_starts_y[s, d], PY))
                 for j in range(min(TILES, lanes_x)):
                     cells = [edge_land[k, s, d, j, c].astype(F32) for c in range(CLASSES)]
-                    terms = [(cells[e + 1] - cells[0]) * along for e in range(DIFFS)]
-                    for b in range(j, lanes_x, TILES):
-                        for e in range(DIFFS):
-                            term = terms[e] * edge_plane_ref[s, d, b]
-                            rims[s, b, e] = rims[s, b, e] + term if d else term
+                    for o in range(len(same_y)):
+                        terms = [(cells[e + 1] - cells[0]) * along[o] for e in range(DIFFS)]
+                        for b in range(j, lanes_x, TILES):
+                            for e in range(DIFFS):
+                                term = terms[e] * edge_plane_ref[s, d, b]
+                                rims[s, o, b, e] = rims[s, o, b, e] + term if d else term
         turn = [lax.rem(2 * BZ - first * RIM - jnp.where(side, 0, RIM), BZ) for side in low]
         rims = {at: pltpu.roll(total, turn[at[0]], 1) for at, total in rims.items()}
         for j in range(min(TILES, lanes_x)):
             for t in range(ROWS):
                 y = t * STEP + k
                 totals = {}
-                for b in range(j, lanes_x, TILES):
-                    for e in range(DIFFS):
-                        total = 0.0
-                        for s in range(len(sides)):
-                            rim = pltpu.roll(rims[s, b, e], BZ - t * RIM, 1) if t else rims[s, b, e]
-                            total = jnp.where(rim_lane[s], rim, total)
-                        totals[b, e] = total
-                for d in range(lanes_y):
-                    if d:
-                        cells = [rows_land[k, d, j, t * CLASSES + c].astype(F32) for c in range(CLASSES)]
-                    else:
-                        cells = [rows[k, place_y, j, t * CLASSES + c].astype(F32) for c in range(CLASSES)]
-                    along = row_along_ref[d, pl.ds(y, 1)]
-                    terms = [(cells[e + 1] - cells[0]) * along for e in range(DIFFS)]
+                for o in range(len(same_y)):
                     for b in range(j, lanes_x, TILES):
                         for e in range(DIFFS):
-                            totals[b, e] = totals[b, e] + terms[e] * row_plane_ref[d, b]
-                for (b, e), total in totals.items():
-                    sums[k, b, t, e] = total
-        hop(0, k)
-
-    def take(k, way, b):
-        settle(sums_land.at[k, way, b], sums_in.at[k, way, b])
+                            total = 0.0
+                            for s in range(len(sides)):
+                                rim = rims[s, o, b, e]
+                                rim = pltpu.roll(rim, BZ - t * RIM, 1) if t else rim
+                                total = jnp.where(rim_lane[s], rim, total)
+                            totals[o, b, e] = total
+                for d in range(2):
+                    if d:
+                        cells = [rows_land[k, j, t * CLASSES + c].astype(F32) for c in range(CLASSES)]
+                    else:
+                        cells = [rows[k, side_y, j, t * CLASSES + c].astype(F32) for c in range(CLASSES)]
+                    for o in range(len(same_y)):
+                        along = row_along_ref[o, d, pl.ds(y, 1)]
+                        terms = [(cells[e + 1] - cells[0]) * along for e in range(DIFFS)]
+                        for b in range(j, lanes_x, TILES):
+                            for e in range(DIFFS):
+                                totals[o, b, e] = totals[o, b, e] + terms[e] * row_plane_ref[d, b]
+                for (o, b, e), total in totals.items():
+                    if o:
+                        halves[k, o - 1, b, t, e] = total
+                    else:
+                        sums[k, b, t, e] = total
+        for o in range(1, len(same_y)):
+            remote(
+                halves.at[k, o - 1], halves_land.at[k, o - 1], halves_out.at[k], halves_in.at[k], {"gy": same_y[o]}
+            )
+
+    def add(k, b, other):
         for t in range(ROWS):
             for e in range(DIFFS):
-                sums[k, b, t, e] = sums[k, b, t, e] + sums_land[k, way, b, t, e]
-
-    def hop(h, k):
-        for way in range(2):
-            @pl.when(place_x == (lanes_x - 1 - h if way else h))
-            def _():
-                past = range(lanes_x - 1 - h) if way else range(lanes_x - 1, h, -1)
-                there = place_x - 1 if way else place_x + 1
-                for b in past:
-                    if h:
-                        take(k, way, b)
+                sums[k, b, t, e] = sums[k, b, t, e] + other[t, e]
+
+    def join_y(k):
+        settle(halves_land.at[k], halves_in.at[k])
+        for o in range(1, len(same_y)):
+            for b in range(lanes_x):
+                add(k, b, halves_land.at[k, o - 1, b])
+        for side in range(2):
+            for b in range(lanes_x) if side else range(lanes_x - 1, -1, -1):
+                @pl.when((side_x == side) & (b < place_x if side else b > place_x))
+                def _():
+                    there = place_x + 1 - 2 * side
+                    remote(sums.at[k, b], pair_land.at[k, b], pair_out.at[k], pair_in.at[k, b], {"gx": there})
+
+    def cross_x(k):
+        for side in range(2):
+            for b in range(lanes_x - 1, -1, -1) if side else range(lanes_x):
+                @pl.when((side_x == side) & (b > place_x if side else b < place_x))
+                def _():
+                    settle(pair_land.at[k, b], pair_in.at[k, b])
+                    add(k, b, pair_land.at[k, b])
                     remote(
-                        sums.at[k, b], sums_land.at[k, way, b], sums_out.at[k], sums_in.at[k, way, b], {"gx": there}
+                        sums.at[k, b], cross_land.at[k, pair_x], cross_out.at[k], cross_in.at[k, pair_x], {"gx": b}
                     )
 
     def write(y, totals):
@@ -370,42 +415,44 @@
             write(t * STEP + Y_FIRST + k, totals)
 
     def finish_y(k):
-        @pl.when(place_x > 0)
-        def _():
-            take(k, 0, place_x)
-
-        @pl.when(place_x < lanes_x - 1)
-        def _():
-            take(k, 1, place_x)
-
+        settle(pair_land.at[k, place_x], pair_in.at[k, place_x])
+        others = [pair_land.at[k, place_x]]
+        for o in range(1, lanes_x // 2):
+            g = lax.rem(pair_x + o, lanes_x // 2)
+            settle(cross_land.at[k, g], cross_in.at[k, g])
+            others.append(cross_land.at[k, g])
         for t in range(ROWS):
-            write(t * STEP + k, [sums[k, place_x, t, e] for e in range(DIFFS)])
-
-    for i in range(max(X_FIRST, Y_FIRST) + lanes_x):
-        if i < Y_FIRST:
-            blend_y(i)
-        if i < X_FIRST:
-            blend_x(i)
-        for h in range(1, lanes_x - 1):
-            if 0 <= i - h + 1 < Y_FIRST:
-                hop(h, i - h + 1)
-        if 0 <= i - 1 < X_FIRST:
-            finish_x(i - 1)
-        if 0 <= i - lanes_x + 2 < Y_FIRST:
-            finish_y(i - lanes_x + 2)
+            totals = []
+            for e in range(DIFFS):
+                total = sums[k, place_x, t, e]
+                for other in others:
+                    total = total + other[t, e]
+                totals.append(total)
+            write(t * STEP + k, totals)
+
+    for event, k in events(send_x, blend_y, blend_x, join_y, cross_x, finish_x, finish_y):
+        event(k)
 
     for k in range(X_FIRST):
         settle(land[k].at[pl.ds(1, lanes_x - 1)], cells_out.at[k])
         settle(rim_land.at[k], rims_out.at[k])
         settle(parts_land.at[k, pl.ds(1, lanes_y - 1)], parts_out.at[k])
     for k in range(Y_FIRST):
-        settle(rows_land.at[k, pl.ds(1, lanes_y - 1)], rows_out.at[k])
+        settle(rows_land.at[k], rows_out.at[k])
         settle(edge_land.at[k], edges_out.at[k])
-        settle(sums.at[k, pl.ds(0, lanes_x - 1)], sums_out.at[k])
+        settle(halves_land.at[k], halves_out.at[k])
+    for x in range(lanes_x):
+        @pl.when(place_x == x)
+        def _():
+            paired = x if x % 2 else lanes_x - 1 - x
+            crossed = lanes_x - 1 - paired
+            for k in range(Y_FIRST):
+                settle(sums.at[k, pl.ds(0, paired)], pair_out.at[k])
+                if crossed:
+                    settle(sums.at[k, pl.ds(0, crossed)], cross_out.at[k])
 
 
 VMEM = pl.BlockSpec(memory_space=pltpu.VMEM)
-SMEM = pl.BlockSpec(memory_space=pltpu.SMEM)
 
 
 def per_device(patch_logits, patch_start, patch_owner):
@@ -418,9 +465,11 @@
     probs = pl.pallas_call(
         functools.partial(blend_kernel, lanes_x, lanes_y, lanes_z),
         out_shape=pltpu.VMEM((BY, CLASSES, BX, BZ), F32),
-        in_specs=[SMEM, SMEM, pl.BlockSpec(memory_space=pl.ANY)],
+        in_specs=[pl.BlockSpec(memory_space=pl.ANY)] * 3,
         out_specs=VMEM,
         scratch_shapes=[
+            pltpu.SMEM((lanes_x, 3, lanes_z, lanes_y), jnp.int32),
+            pltpu.SMEM((lanes_x, lanes_z, lanes_y), jnp.int32),
             pltpu.VMEM((PX, lines), BF16),
             pltpu.VMEM((lines // BZ, PX, BZ), BF16),
             pltpu.VMEM((PHASES, 2 * BZ, 2 * BZ), BF16),
@@ -428,22 +477,28 @@
             pltpu.VMEM((X_FIRST, sides, lanes_x, CLASSES, BX, BZ), BF16),
             pltpu.VMEM((X_FIRST, lanes_y, ROWS, DIFFS, BX, BZ), F32),
             pltpu.VMEM((X_FIRST, lanes_y, ROWS, DIFFS, BX, BZ), F32),
-            pltpu.VMEM((Y_FIRST, lanes_y, TILES, ROWS * CLASSES, BX, BZ), BF16),
-            pltpu.VMEM((Y_FIRST, lanes_y, TILES, ROWS * CLASSES, BX, BZ), BF16),
-            pltpu.VMEM((Y_FIRST, sides, lanes_y, TILES, CLASSES, BX, BZ), BF16),
+            pltpu.VMEM((Y_FIRST, 2, TILES, ROWS * CLASSES, BX, BZ), BF16),
+            pltpu.VMEM((Y_FIRST, TILES, ROWS * CLASSES, BX, BZ), BF16),
+            pltpu.VMEM((Y_FIRST, sides, 2, TILES, CLASSES, BX, BZ), BF16),
             pltpu.VMEM((Y_FIRST, lanes_x, ROWS, DIFFS, BX, BZ), F32),
-            pltpu.VMEM((Y_FIRST, 2, lanes_x, ROWS, DIFFS, BX, BZ), F32),
+            pltpu.VMEM((Y_FIRST, lanes_y // 2 - 1, lanes_x, ROWS, DIFFS, BX, BZ), F32),
+            pltpu.VMEM((Y_FIRST, lanes_y // 2 - 1, lanes_x, ROWS, DIFFS, BX, BZ), F32),
+            pltpu.VMEM((Y_FIRST, lanes_x, ROWS, DIFFS, BX, BZ), F32),
+            pltpu.VMEM((Y_FIRST, lanes_x // 2, ROWS, DIFFS, BX, BZ), F32),
             pltpu.VMEM((lanes_x, lanes_y * BY, BZ), F32),
             pltpu.VMEM((lanes_x, BX, BZ), F32),
             pltpu.VMEM((sides, lanes_x, BX, BZ), F32),
-            pltpu.VMEM((lanes_y, BY, BZ), F32),
-            pltpu.VMEM((lanes_y, lanes_x, BX, BZ), F32),
-            pltpu.VMEM((sides, lanes_y, lanes_x, BX, BZ), F32),
+            pltpu.VMEM((lanes_y // 2, 2, BY, BZ), F32),
+            pltpu.VMEM((2, lanes_x, BX, BZ), F32),
+            pltpu.VMEM((sides, 2, lanes_x, BX, BZ), F32),
             pltpu.VMEM((BY, BX, BZ), F32),
+            dma((2,)),
             dma((PY // STEP,)),
             *[dma((X_FIRST,))] * 6,
-            *[dma((Y_FIRST,))] * 5,
-            dma((Y_FIRST, 2, lanes_x)),
+            *[dma((Y_FIRST,))] * 7,
+            dma((Y_FIRST, lanes_x)),
+            dma((Y_FIRST,)),
+            dma((Y_FIRST, lanes_x // 2)),
             *[pltpu.VMEM((lanes_x, MAIN, BX, BZ), BF16)] * X_FIRST,
         ],
         compiler_params=pltpu.CompilerParams(collective_id=0, has_side_effects=True),

time: 39.1 us -> 36.7 us (0.939)
  Pallas kernels: 38 us -> 35.6 us
    pallas_call x1, Pallas kernels: 38 us -> 35.6 us  [per_device(): pl.pallas_call(functools.partial(blend_kernel, lanes_x, lanes_y, lanes_z)...]
where the time goes in v2:
time: 36.7 us; the launch traced here: 36.5 us
  Pallas kernels  35.6 us (97%)
  local copies, waits for them, and re-layouts  0.82 us (2%)
    pallas_call x1, Pallas kernels, per_device(): pl.pallas_call(functools.partial(blend_kernel, lanes_x, lanes_y, lanes_z)...  35.6 us
    transpose x1, local copies, waits for them, and re-layouts, per_device(): return jnp.transpose(probs, (2, 0, 1, 3))  0.82 us

profile of v2, /device:TPU:0, one launch (start us, length us, event | category | flops | bytes accessed | tf_op | source)
XLA Modules:
  0.0 36.5 jit_solution(18304069612891541717)
XLA Ops:
  0.0 35.6 %shard_map.37 = f32[32,3,8,128]{3,2,1,0:T(8,128)S(1)} custom-call(s32[4,3,2,4]{3,2,1,0:T(2,128)} %bitcast.6, s32[4,2,4]{2,1,0:T(2,128)} %bitcast.7, bf16[24,20736]{1,0:T(8,128)(2,1)} %bitcast.5), custom_call_target="tpu_custom_call" | custom-call | tf_op jit(solution)/shard_map/pallas_call | solution.py:465
  35.6 0.8 %copy.4 = f32[8,32,3,128]{3,1,2,0:T(8,128)} copy(f32[8,32,3,128]{3,0,2,1:T(8,128)S(1)} %bitcast.4) | data formatting | bytes 786432 | tf_op jit(solution)/shard_map/transpose | solution.py:510

commit v3 on v1

--- a/solution.py
+++ b/solution.py
@@ -25,8 +25,9 @@
 SPAN = SLOTS * STEP
 GROUP = STEP * CLASSES * PZ
 PHASES = BZ // RIM
-Y_FIRST = 4
+Y_FIRST = 3
 X_FIRST = STEP - Y_FIRST
+EARLY = ((0, 1), (0, 1), (0,), (), (),)
 MESH = pl.DeviceIdType.MESH
 F32 = jnp.float32
 BF16 = jnp.bfloat16
@@ -42,12 +43,12 @@
 
 def blend_kernel(
     lanes_x, lanes_y, lanes_z,
-    start_ref, owner_ref, logits_ref, out_ref,
-    raw_ref, cells_ref, move_ref, packed, rim_land, parts, parts_land,
-    rows, rows_land, edge_land, sums, sums_land,
+    starts_ref, owners_ref, logits_ref, out_ref,
+    start_ref, owner_ref, raw_ref, cells_ref, move_ref, packed, rim_land, parts, parts_land,
+    rows, rows_land, edge_land, sums, pair_land, cross_land,
     along_ref, plane_ref, rim_plane_ref, row_along_ref, row_plane_ref, edge_plane_ref, weight_ref,
-    raw_in, cells_out, cells_in, rims_out, rims_in, parts_out, parts_in,
-    rows_out, rows_in, edges_out, edges_in, sums_out, sums_in,
+    table_in, raw_in, cells_out, cells_in, rims_out, rims_in, parts_out, parts_in,
+    rows_out, rows_in, edges_out, edges_in, pair_out, pair_in, cross_out, cross_in,
     *land,
 ):
     place_x = lax.axis_index("gx")
@@ -65,13 +66,20 @@
     def settle(ref, sem):
         pltpu.make_async_copy(ref, ref, sem).wait()
 
+    side_x = lax.rem(place_x, 2)
+    pair_x = place_x // 2
+    tables = [
+        pltpu.make_async_copy(starts_ref, start_ref, table_in.at[0]),
+        pltpu.make_async_copy(owners_ref, owner_ref, table_in.at[1]),
+    ]
+    for table in tables:
+        table.start()
     barrier = pltpu.get_barrier_semaphore()
-    peers = [{"gz": ahead(place_z, s, lanes_z)} for s in sides]
-    for axis, place, size in (("gx", place_x, lanes_x), ("gy", place_y, lanes_y)):
-        for d in range(1, size):
-            there = {axis: ahead(place, d, size)}
-            peers.append(there)
-            peers += [{**there, "gz": ahead(place_z, s, lanes_z)} for s in sides]
+    near = [{"gx": ahead(place_x, d, lanes_x)} for d in range(1, lanes_x)]
+    near += [{"gy": ahead(place_y, d, lanes_y)} for d in range(1, lanes_y)]
+    peers = list(near)
+    for there in near + [{}]:
+        peers += [{**there, "gz": ahead(place_z, s, lanes_z)} for s in sides]
     for peer in peers:
         pl.semaphore_signal(barrier, inc=1, device_id=peer, device_id_type=MESH)
 
@@ -82,6 +90,8 @@
         loads.append(pltpu.make_async_copy(logits_ref.at[:, lanes], raw_ref.at[:, lanes], raw_in.at[g]))
         loads[-1].start()
 
+    for table in tables:
+        table.wait()
     code = owner_ref[place_x, place_z, place_y]
     start_x, start_y, start_z = corner_of(code, place_z)
     shift_z = place_z * BZ - start_z
@@ -151,18 +161,23 @@
             src_ref=src, dst_ref=dst, send_sem=send, recv_sem=recv, device_id=where, device_id_type=MESH
         ).start()
 
-    def send_x(k):
+    middle = jnp.where((place_x > 0) & (place_x < lanes_x - 1), 1, 0)
+
+    def send_x(k, side):
         r = Y_FIRST + k
-        for d in far_x + [0]:
-            there = ahead(place_x, d, lanes_x)
-            tile = lax.rem(there, TILES)
-            if d:
-                cells = packed.at[r, tile, pl.ds(0, MAIN)]
-                remote(cells, land[k].at[d], cells_out.at[k], cells_in.at[k], {"gx": there})
-            rims = packed.at[r, tile, pl.ds(MAIN, CLASSES)]
-            for s, step in enumerate(sides):
-                where = {"gx": there, "gz": ahead(place_z, step, lanes_z)}
-                remote(rims, rim_land.at[k, s, d], rims_out.at[k], rims_in.at[k], where)
+
+        @pl.when(middle == side)
+        def _():
+            for d in far_x + [0]:
+                there = ahead(place_x, d, lanes_x)
+                tile = lax.rem(there, TILES)
+                if d:
+                    cells = packed.at[r, tile, pl.ds(0, MAIN)]
+                    remote(cells, land[k].at[d], cells_out.at[k], cells_in.at[k], {"gx": there})
+                rims = packed.at[r, tile, pl.ds(MAIN, CLASSES)]
+                for s, step in enumerate(sides):
+                    where = {"gx": there, "gz": ahead(place_z, step, lanes_z)}
+                    remote(rims, rim_land.at[k, s, d], rims_out.at[k], rims_in.at[k], where)
 
     def send_y(k):
         for d in far_y + [0]:
@@ -185,7 +200,8 @@
             pack(Y_FIRST + k)
             if k == 0 and not Y_FIRST:
                 pl.semaphore_wait(barrier, len(peers))
-            send_x(k)
+            for side in EARLY[k]:
+                send_x(k, side)
 
     cell_x = place_x * BX + sub
     cell_z = place_z * BZ + lane
@@ -329,25 +345,30 @@
                             totals[b, e] = totals[b, e] + terms[e] * row_plane_ref[d, b]
                 for (b, e), total in totals.items():
                     sums[k, b, t, e] = total
-        hop(0, k)
-
-    def take(k, way, b):
-        settle(sums_land.at[k, way, b], sums_in.at[k, way, b])
+        pair_up(k)
+
+    def add(k, b, other):
         for t in range(ROWS):
             for e in range(DIFFS):
-                sums[k, b, t, e] = sums[k, b, t, e] + sums_land[k, way, b, t, e]
-
-    def hop(h, k):
-        for way in range(2):
-            @pl.when(place_x == (lanes_x - 1 - h if way else h))
-            def _():
-                past = range(lanes_x - 1 - h) if way else range(lanes_x - 1, h, -1)
-                there = place_x - 1 if way else place_x + 1
-                for b in past:
-                    if h:
-                        take(k, way, b)
+                sums[k, b, t, e] = sums[k, b, t, e] + other[t, e]
+
+    def pair_up(k):
+        for side in range(2):
+            for b in range(lanes_x) if side else range(lanes_x - 1, -1, -1):
+                @pl.when((side_x == side) & (b < place_x if side else b > place_x))
+                def _():
+                    there = place_x + 1 - 2 * side
+                    remote(sums.at[k, b], pair_land.at[k, b], pair_out.at[k], pair_in.at[k, b], {"gx": there})
+
+    def cross_x(k):
+        for side in range(2):
+            for b in range(lanes_x - 1, -1, -1) if side else range(lanes_x):
+                @pl.when((side_x == side) & (b > place_x if side else b < place_x))
+                def _():
+                    settle(pair_land.at[k, b], pair_in.at[k, b])
+                    add(k, b, pair_land.at[k, b])
                     remote(
-                        sums.at[k, b], sums_land.at[k, way, b], sums_out.at[k], sums_in.at[k, way, b], {"gx": there}
+                        sums.at[k, b], cross_land.at[k, pair_x], cross_out.at[k], cross_in.at[k, pair_x], {"gx": b}
                     )
 
     def write(y, totals):
@@ -370,29 +391,48 @@
             write(t * STEP + Y_FIRST + k, totals)
 
     def finish_y(k):
-        @pl.when(place_x > 0)
-        def _():
-            take(k, 0, place_x)
-
-        @pl.when(place_x < lanes_x - 1)
-        def _():
-            take(k, 1, place_x)
-
+        settle(pair_land.at[k, place_x], pair_in.at[k, place_x])
+        others = [pair_land.at[k, place_x]]
+        for o in range(1, lanes_x // 2):
+            g = lax.rem(pair_x + o, lanes_x // 2)
+            settle(cross_land.at[k, g], cross_in.at[k, g])
+            others.append(cross_land.at[k, g])
         for t in range(ROWS):
-            write(t * STEP + k, [sums[k, place_x, t, e] for e in range(DIFFS)])
-
-    for i in range(max(X_FIRST, Y_FIRST) + lanes_x):
-        if i < Y_FIRST:
-            blend_y(i)
-        if i < X_FIRST:
-            blend_x(i)
-        for h in range(1, lanes_x - 1):
-            if 0 <= i - h + 1 < Y_FIRST:
-                hop(h, i - h + 1)
-        if 0 <= i - 1 < X_FIRST:
-            finish_x(i - 1)
-        if 0 <= i - lanes_x + 2 < Y_FIRST:
-            finish_y(i - lanes_x + 2)
+            totals = []
+            for e in range(DIFFS):
+                total = sums[k, place_x, t, e]
+                for other in others:
+                    total = total + other[t, e]
+                totals.append(total)
+            write(t * STEP + k, totals)
+
+    for event, *which in [
+        (blend_y, 0),
+        (blend_x, 0),
+        (send_x, 2, 1),
+        (send_x, 3, 0),
+        (cross_x, 0),
+        (blend_y, 1),
+        (blend_x, 1),
+        (send_x, 4, 0),
+        (send_x, 3, 1),
+        (cross_x, 1),
+        (finish_x, 0),
+        (blend_y, 2),
+        (blend_x, 2),
+        (send_x, 4, 1),
+        (finish_y, 0),
+        (cross_x, 2),
+        (finish_x, 1),
+        (blend_x, 3),
+        (finish_y, 1),
+        (finish_x, 2),
+        (blend_x, 4),
+        (finish_y, 2),
+        (finish_x, 3),
+        (finish_x, 4),
+    ]:
+        event(*which)
 
     for k in range(X_FIRST):
         settle(land[k].at[pl.ds(1, lanes_x - 1)], cells_out.at[k])
@@ -401,11 +441,18 @@
     for k in range(Y_FIRST):
         settle(rows_land.at[k, pl.ds(1, lanes_y - 1)], rows_out.at[k])
         settle(edge_land.at[k], edges_out.at[k])
-        settle(sums.at[k, pl.ds(0, lanes_x - 1)], sums_out.at[k])
+    for x in range(lanes_x):
+        @pl.when(place_x == x)
+        def _():
+            paired = x if x % 2 else lanes_x - 1 - x
+            crossed = lanes_x - 1 - paired
+            for k in range(Y_FIRST):
+                settle(sums.at[k, pl.ds(0, paired)], pair_out.at[k])
+                if crossed:
+                    settle(sums.at[k, pl.ds(0, crossed)], cross_out.at[k])
 
 
 VMEM = pl.BlockSpec(memory_space=pltpu.VMEM)
-SMEM = pl.BlockSpec(memory_space=pltpu.SMEM)
 
 
 def per_device(patch_logits, patch_start, patch_owner):
@@ -418,9 +465,11 @@
     probs = pl.pallas_call(
         functools.partial(blend_kernel, lanes_x, lanes_y, lanes_z),
         out_shape=pltpu.VMEM((BY, CLASSES, BX, BZ), F32),
-        in_specs=[SMEM, SMEM, pl.BlockSpec(memory_space=pl.ANY)],
+        in_specs=[pl.BlockSpec(memory_space=pl.ANY)] * 3,
         out_specs=VMEM,
         scratch_shapes=[
+            pltpu.SMEM((lanes_x, 3, lanes_z, lanes_y), jnp.int32),
+            pltpu.SMEM((lanes_x, lanes_z, lanes_y), jnp.int32),
             pltpu.VMEM((PX, lines), BF16),
             pltpu.VMEM((lines // BZ, PX, BZ), BF16),
             pltpu.VMEM((PHASES, 2 * BZ, 2 * BZ), BF16),
@@ -432,7 +481,8 @@
             pltpu.VMEM((Y_FIRST, lanes_y, TILES, ROWS * CLASSES, BX, BZ), BF16),
             pltpu.VMEM((Y_FIRST, sides, lanes_y, TILES, CLASSES, BX, BZ), BF16),
             pltpu.VMEM((Y_FIRST, lanes_x, ROWS, DIFFS, BX, BZ), F32),
-            pltpu.VMEM((Y_FIRST, 2, lanes_x, ROWS, DIFFS, BX, BZ), F32),
+            pltpu.VMEM((Y_FIRST, lanes_x, ROWS, DIFFS, BX, BZ), F32),
+            pltpu.VMEM((Y_FIRST, lanes_x // 2, ROWS, DIFFS, BX, BZ), F32),
             pltpu.VMEM((lanes_x, lanes_y * BY, BZ), F32),
             pltpu.VMEM((lanes_x, BX, BZ), F32),
             pltpu.VMEM((sides, lanes_x, BX, BZ), F32),
@@ -440,10 +490,13 @@
             pltpu.VMEM((lanes_y, lanes_x, BX, BZ), F32),
             pltpu.VMEM((sides, lanes_y, lanes_x, BX, BZ), F32),
             pltpu.VMEM((BY, BX, BZ), F32),
+            dma((2,)),
             dma((PY // STEP,)),
             *[dma((X_FIRST,))] * 6,
             *[dma((Y_FIRST,))] * 5,
-            dma((Y_FIRST, 2, lanes_x)),
+            dma((Y_FIRST, lanes_x)),
+            dma((Y_FIRST,)),
+            dma((Y_FIRST, lanes_x // 2)),
             *[pltpu.VMEM((lanes_x, MAIN, BX, BZ), BF16)] * X_FIRST,
         ],
         compiler_params=pltpu.CompilerParams(collective_id=0, has_side_effects=True),

time: 39.1 us -> 35 us (0.90)
  Pallas kernels: 38 us -> 33.9 us
    pallas_call x1, Pallas kernels: 38 us -> 33.9 us  [per_device(): pl.pallas_call(functools.partial(blend_kernel, lanes_x, lanes_y, lanes_z)...]
where the time goes in v3:
time: 35 us; the launch traced here: 34.8 us
  Pallas kernels  33.9 us (97%)
  local copies, waits for them, and re-layouts  0.82 us (2%)
    pallas_call x1, Pallas kernels, per_device(): pl.pallas_call(functools.partial(blend_kernel, lanes_x, lanes_y, lanes_z)...  33.9 us
    transpose x1, local copies, waits for them, and re-layouts, per_device(): return jnp.transpose(probs, (2, 0, 1, 3))  0.82 us

profile of v3, /device:TPU:0, one launch (start us, length us, event | category | flops | bytes accessed | tf_op | source)
XLA Modules:
  0.0 34.8 jit_solution(14693740619642627023)
XLA Ops:
  0.0 33.9 %shard_map.37 = f32[32,3,8,128]{3,2,1,0:T(8,128)S(1)} custom-call(s32[4,3,2,4]{3,2,1,0:T(2,128)} %bitcast.6, s32[4,2,4]{2,1,0:T(2,128)} %bitcast.7, bf16[24,20736]{1,0:T(8,128)(2,1)} %bitcast.5), custom_call_target="tpu_custom_call" | custom-call | tf_op jit(solution)/shard_map/pallas_call | solution.py:465
  33.9 0.8 %copy.4 = f32[8,32,3,128]{3,1,2,0:T(8,128)} copy(f32[8,32,3,128]{3,0,2,1:T(8,128)S(1)} %bitcast.4) | data formatting | bytes 786432 | tf_op jit(solution)/shard_map/transpose | solution.py:508
